TPU v7x, 512 devices: a whole 4x4x16 slice. The times are simulated.
512 devices in a mesh: src: 8 (over x, core), tgt: 64 (over y, z).
Axes of the slice: x: 4, y: 4, z: 16, core: 2. Of those that a mesh axis runs over, the one named last changes fastest.
Arguments:
- source_points: float32 [32, 16384], P(None, ('src', 'tgt')), may hold values from -1.25 to 1.25
- target_points: float32 [32, 65536], P('src', 'tgt'), may hold values from -1.2 to 1.2
- source_potential: float32 [16384], P(('src', 'tgt')), may hold values from -1.5 to 1.5
- target_potential: float32 [65536], P('tgt'), may hold values from -1.5 to 1.5
- source_weight: float32 [16384], P(('src', 'tgt')), may hold values from 0.5 to 2
- target_weight: float32 [65536], P('tgt'), may hold values from 0.5 to 2
- core_previous: float32 [34, 34], replicated, may hold values from -0.12 to 0.12
Outputs:
- source_new: float32 [16384], P(('src', 'tgt'))
- target_new: float32 [65536], P('tgt')
- core_new: float32 [34, 34], replicated
All inputs are finite; a program needn't handle non-finite values.
Results may differ from a plain program's by a relative error of at most 0.0002.
Values sent between devices are 32-bit elements; how exact they have to be, the bound alone decides.
No kernel may reach another device: no remote copies, remote signals or barrier semaphores. Data moves between devices by JAX's collectives and lax.ppermute only.
A program may use at most 64 MiB of HBM per device.

v0:
```python
import functools
import jax
import jax.numpy as jnp
from jax import lax
from jax.sharding import Mesh
from jax.sharding import PartitionSpec as P

TGT = ("tgt_0", "tgt_1")
SRC = ("src_0", "src_1")
SRC_TGT = ("src_0", "src_1", "tgt_0", "tgt_1")
EPSILON = 0.5
HIGHEST = lax.Precision.HIGHEST


def rows_first(arrays, axis, dims):
    turned = [jnp.moveaxis(a, dim, 0) for a, dim in zip(arrays, dims)]
    both = jnp.concatenate([t.reshape(len(t), -1) for t in turned], axis=1)
    filled, at, gathered = (lax.all_gather(both, axis, axis=0, tiled=True), 0, [])
    for t, dim in zip(turned, dims):
        slab = filled[:, at : at + t[0].size].reshape(-1, *t.shape[1:])
        gathered.append(jnp.moveaxis(slab, 0, dim))
        at += t[0].size
    return tuple(gathered)


def sent_to_all(x, axis):
    copies = jnp.broadcast_to(x, (lax.axis_size(axis), *x.shape))
    return lax.all_to_all(copies, axis, split_axis=0, concat_axis=0, tiled=True)


def laid_out(parts, dim):
    parts = jnp.moveaxis(parts, 0, dim)
    dims = parts.shape
    return parts.reshape(*dims[:dim], dims[dim] * dims[dim + 1], *dims[dim + 2 :])


def collect(x, axis, dim):
    parts = sent_to_all(x, axis)
    return laid_out(parts, dim)


def by_axis(x, axes):
    return functools.reduce(lax.psum, axes, x)


def collected_together(x, axis):
    leaves = jax.tree.leaves(x)
    sequence = sorted(range(len(leaves)), key=lambda k: -leaves[k].size)
    width = (1, *leaves[sequence[0]].shape)[-1]
    lines = [
        jnp.pad(leaves[k].reshape(-1), (0, -leaves[k].size % width)).reshape(-1, width)
        for k in sequence
    ]
    both, at, found = (lax.all_gather(jnp.concatenate(lines), axis), 0, {})
    for k, line in zip(sequence, lines):
        slab = both[:, at : at + len(line)].reshape(len(both), -1)
        found[k] = slab[:, : leaves[k].size].reshape(-1, *leaves[k].shape)
        at += len(line)
    numbers = iter(range(len(leaves)))
    return jax.tree.map(lambda _: found[next(numbers)], x)


def joined_all(x, axes, combine):
    for axis in axes:
        pieces = collected_together(x, axis)
        x = jax.tree.map(lambda part: part[0], pieces)
        for k in range(1, lax.axis_size(axis)):
            x = combine(x, jax.tree.map(lambda part: part[k], pieces))
    return x


def all_in_one(x, axis):
    leaves = jax.tree.leaves(x)
    sequence = sorted(range(len(leaves)), key=lambda k: -leaves[k].size)
    width = (1, *leaves[sequence[0]].shape)[-1]
    lines = [
        jnp.pad(leaves[k].reshape(-1), (0, -leaves[k].size % width)).reshape(-1, width)
        for k in sequence
    ]
    both, at, found = (sent_to_all(jnp.concatenate(lines), axis), 0, {})
    for k, line in zip(sequence, lines):
        slab = both[:, at : at + len(line)].reshape(len(both), -1)
        found[k] = slab[:, : leaves[k].size].reshape(-1, *leaves[k].shape)
        at += len(line)
    numbers = iter(range(len(leaves)))
    return jax.tree.map(lambda _: found[next(numbers)], x)


def combined_pairwise(pieces, combine):
    while len(jax.tree.leaves(pieces)[0]) > 1:
        pieces = jax.vmap(combine)(
            *(jax.tree.map(lambda part: part[side::2], pieces) for side in (0, 1))
        )
    return jax.tree.map(lambda part: part[0], pieces)


def combined_all(x, axis, combine):
    pieces = all_in_one(x, axis)
    return combined_pairwise(pieces, combine)


def factors(points):
    squares = jnp.sum(points * points, axis=0, keepdims=True)
    unit_row = jnp.ones_like(squares)
    return (
        jnp.concatenate([squares, unit_row, -2.0 * points], 0),
        jnp.concatenate([unit_row, squares, points], 0),
    )


def contract_rank(left_block, weighted):
    return lax.dot_general(
        left_block,
        weighted,
        (((0,), (0,)), ((), ())),
        precision=HIGHEST,
        preferred_element_type=jnp.float32,
    )


def contract_last(former, latter):
    return lax.dot_general(
        former,
        latter,
        (((1,), (1,)), ((), ())),
        precision=HIGHEST,
        preferred_element_type=jnp.float32,
    )


def row_blocks(values, block_size):
    number = values.shape[-1] // block_size
    shaped = values.reshape(values.shape[:-1] + (number, block_size))
    return jnp.moveaxis(shaped, -2, 0)


def combine_parts(former, latter):
    highest = jnp.maximum(former[0], latter[0])
    return (
        highest,
        former[1] * jnp.exp(former[0] - highest) + latter[1] * jnp.exp(latter[0] - highest),
    )


def on_device(
    source_points,
    target_points,
    source_potential,
    target_potential,
    source_weight,
    target_weight,
    core_previous,
):
    spread = lax.axis_size(TGT)
    sources = source_points.shape[1] * spread * lax.axis_size(SRC)
    targets = target_potential.shape[0] * spread
    points, potential, weight = rows_first(
        (source_points, source_potential, source_weight), TGT, (1, 0, 0)
    )
    features = collect(target_points, SRC, 0)
    log_source = jnp.log(weight) - jnp.log(jnp.float32(sources))
    log_target = jnp.log(target_weight) - jnp.log(jnp.float32(targets))
    left_source, right_source = factors(points)
    left_target, right_target = factors(features)
    row_count = points.shape[1]
    share_count = row_count // spread
    block_size = min(512, row_count)
    left_blocks = row_blocks(left_source, block_size)
    right_blocks = row_blocks(right_source, block_size)
    potential_blocks = row_blocks(potential, block_size)
    weight_blocks = row_blocks(log_source, block_size)
    rank_size = left_source.shape[0]
    previous_w = jnp.dot(core_previous, left_target, precision=HIGHEST)

    def plan_step(running, portion):
        left_block, right_block, source_part, log_weight = portion
        scores = contract_rank(left_block, previous_w)
        plan_tile = jnp.exp(
            log_weight[:, None]
            + log_target[None, :]
            + (source_part[:, None] + target_potential[None, :] + 2.0 * scores) / EPSILON
        )
        carried = contract_last(right_target, plan_tile)
        return (running + contract_last(right_block, carried), None)

    partial_core, _ = lax.scan(
        plan_step,
        jnp.zeros((rank_size, rank_size), jnp.float32),
        (left_blocks, right_blocks, potential_blocks, weight_blocks),
    )
    core_new = by_axis(partial_core, SRC_TGT)
    current = jnp.dot(core_new, left_target, precision=HIGHEST)

    def row_step(left_block):
        scores = (
            log_target[None, :]
            + (target_potential[None, :] + 2.0 * contract_rank(left_block, current)) / EPSILON
        )
        maxima = jnp.max(scores, axis=1)
        return (maxima, jnp.sum(jnp.exp(scores - maxima[:, None]), axis=1))

    local_max, local_sum = lax.map(row_step, left_blocks)
    local_max = local_max.reshape(row_count)
    local_sum = local_sum.reshape(row_count)
    offset = lax.axis_index(TGT) * share_count
    highest, summed = joined_all((local_max, local_sum), TGT, combine_parts)
    source_new = EPSILON * (log_source - highest - jnp.log(summed))
    own_rows = lax.dynamic_slice_in_dim(source_new, offset, share_count)
    new_blocks = row_blocks(source_new, block_size)

    def column_step(state, portion):
        maxima, totals = state
        left_block, log_weight, source_part = portion
        scores = (
            log_weight[:, None]
            + (source_part[:, None] + 2.0 * contract_rank(left_block, current)) / EPSILON
        )
        highest = jnp.maximum(maxima, jnp.max(scores, axis=0))
        totals = totals * jnp.exp(maxima - highest) + jnp.sum(
            jnp.exp(scores - highest[None, :]), axis=0
        )
        return ((highest, totals), None)

    columns = target_potential.shape[0]
    start = (jnp.full((columns,), -jnp.inf, jnp.float32), jnp.zeros((columns,), jnp.float32))
    (column_max, column_total), _ = lax.scan(
        column_step, start, (left_blocks, weight_blocks, new_blocks)
    )
    highest, summed = combined_all((column_max, column_total), SRC, combine_parts)
    target_new = EPSILON * (log_target - highest - jnp.log(summed))
    return (own_rows, target_new, core_new)


def solution(mesh):
    finer = Mesh(mesh.devices.reshape(4, 2, 4, 16), ("src_0", "src_1", "tgt_0", "tgt_1"))
    placed = (P(None, SRC_TGT), P(SRC, TGT), P(SRC_TGT), P(TGT), P(SRC_TGT), P(TGT), P())
    return jax.shard_map(
        on_device, mesh=finer, in_specs=placed, out_specs=(P(SRC_TGT), P(TGT), P()), check_vma=False
    )
```

profile of v0, /device:TPU:1, one launch (start us, length us, event | category | flops | bytes accessed | tf_op | source)
XLA Modules:
  0.0 303.7 jit_solution(410053554644530980)
XLA Ops:
  0.6 1.4 broadcast_in_dim.44
  2.0 10.1 %all-to-all-start = ((f32[8,4,1024]{2,1,0:T(4,128)}), f32[8,4,1024]{2,1,0:T(4,128)S(1)}, u32[]{:S(2)}, u32[]{:S(2)}) async-start(f32[8,4,1024]{2,1,0:T(4,128)} %broadcast_in_dim.44), calls=%async_computation | async-start | bytes 262144 | tf_op jit(solution)/shard_map/all_to_all | solution.py:28
  12.1 0.8 copy.36
  12.9 0.7 copy.37
  13.7 0.7 copy.38
  14.5 77.8 %all_gather.15 = f32[2048,34]{1,0:T(8,128)S(1)} all-gather(f32[32,34]{1,0:T(8,128)S(1)} %pad_maximum_fusion.4), channel_id=1, replica_groups=mesh['src_0'=4,'src_1'=2,'tgt_0'=4,'tgt_1'=16] {'tgt_0','tgt_1'}, dimensions={0}, use_global_device_ids=true | all-gather | bytes 282880 | tf_op jit(solution)/shard_map/all_gather | solution.py:18
  92.2 1.2 slice_reduce_fusion
  94.7 0.3 convolution_bitcast_fusion
  95.0 19.5 %while.37 = (s32[]{:T(128)}, f32[34,34]{1,0:T(8,128)S(1)}, f32[4,34,512]{2,0,1:T(4,128)S(1)}, f32[4,512]{1,0:T(4,128)S(1)}, f32[1024]{0:T(1024)S(1)}, /*index=5*...) while((s32[]{:T(128)}, f32[34,34]{1,0:T(8,128)S(1)}, ...), condition=%wide.region_3.4_spmd.clone, body=%wide.region_2.3_spmd.clone.sunk | while | flops 438069504 | bytes 4957355 | solution.py:186
  95.0 1.9 fusion.110
  96.9 2.7 fusion.111
  99.9 1.9 fusion.110
  101.8 2.7 fusion.111
  104.8 1.9 fusion.110
  106.7 2.7 fusion.111
  109.7 1.9 fusion.110
  111.5 2.7 fusion.111
  114.5 13.5 %psum.28 = f32[34,34]{1,0:T(8,128)S(1)} all-reduce(f32[34,34]{1,0:T(8,128)S(1)} %get-tuple-element.131), channel_id=1, replica_groups=mesh['src_0'=4,'src_1'=2,'tgt_0'=4,'tgt_1'=16] {'src_0'}, use_global_device_ids=true, to_apply=%region_4.5 | all-reduce | flops 1156 | bytes 9248 | tf_op jit(solution)/shard_map/psum | solution.py:43
  128.0 32.6 %psum.29 = f32[34,34]{1,0:T(8,128)S(1)} all-reduce(f32[34,34]{1,0:T(8,128)S(1)} %psum.28), channel_id=1, replica_groups=mesh['src_0'=4,'src_1'=2,'tgt_0'=4,'tgt_1'=16] {'src_1'}, use_global_device_ids=true, to_apply=%region_5.6 | all-reduce | flops 1156 | bytes 9248 | tf_op jit(solution)/shard_map/psum | solution.py:43
  160.7 12.5 %psum.30 = f32[34,34]{1,0:T(8,128)S(1)} all-reduce(f32[34,34]{1,0:T(8,128)S(1)} %psum.29), channel_id=1, replica_groups=mesh['src_0'=4,'src_1'=2,'tgt_0'=4,'tgt_1'=16] {'tgt_0'}, use_global_device_ids=true, to_apply=%region_6.7 | all-reduce | flops 1156 | bytes 9248 | tf_op jit(solution)/shard_map/psum | solution.py:43
  173.2 39.7 %psum.31 = f32[34,34]{1,0:T(8,128)S(1)} all-reduce(f32[34,34]{1,0:T(8,128)S(1)} %psum.30), channel_id=1, replica_groups=mesh['src_0'=4,'src_1'=2,'tgt_0'=4,'tgt_1'=16] {'tgt_1'}, use_global_device_ids=true, to_apply=%region_7.8 | all-reduce | flops 1156 | bytes 9248 | tf_op jit(solution)/shard_map/psum | solution.py:43
  213.5 11.3 %while.36 = (s32[]{:T(128)}, f32[4,512]{1,0:T(4,128)S(1)}, f32[4,512]{1,0:T(4,128)S(1)}, f32[1024]{0:T(1024)S(1)}, f32[1024]{0:T(1024)S(1)}, /*index=5*/f32[4,34...) while((s32[]{:T(128)}, f32[4,512]{1,0:T(4,128)S(1)}, f32[4,512]{1,0:T(4,128)S(1)}, ...), condition=%wide.region_11.12_spmd, body=%wide.region_8.11_spmd.sunk | while | flops 217578496 | bytes 4462697 | solution.py:202
  213.5 2.2 fusion.104
  215.7 0.5 exponential_reduce_fusion.4
  216.3 2.2 fusion.104
  218.5 0.5 exponential_reduce_fusion.4
  219.1 2.2 fusion.104
  221.3 0.5 exponential_reduce_fusion.4
  222.0 2.2 fusion.104
  224.2 0.5 exponential_reduce_fusion.4
  224.9 9.0 %all-gather.2 = f32[4,2,2048]{2,1,0:T(2,128)S(1)} all-gather(f32[1,2,2048]{2,1,0:T(2,128)S(1)} %maximum_bitcast_fusion.2), channel_id=2, replica_groups=mesh['src_0'=4,'src_1'=2,'tgt_0'=4,'tgt_1'=16] {'tgt_0'}, dimensions={0}, use_global_device_ids=true | all-gather | bytes 81920 | tf_op jit(solution)/shard_map/all_gather | solution.py:54
  233.9 20.8 %all-gather.3 = f32[16,2,2048]{2,1,0:T(2,128)S(1)} all-gather(f32[1,2,2048]{2,1,0:T(2,128)S(1)} %maximum_bitcast_fusion.3), channel_id=3, replica_groups=mesh['src_0'=4,'src_1'=2,'tgt_0'=4,'tgt_1'=16] {'tgt_1'}, dimensions={0}, use_global_device_ids=true | all-gather | bytes 278528 | tf_op jit(solution)/shard_map/all_gather | solution.py:54
  254.8 0.4 slice_reduce_fusion.16
  255.2 0.3 slice_reduce_fusion.14
  256.2 10.2 %while.38 = (s32[]{:T(128)}, f32[1024]{0:T(1024)S(1)}, f32[1024]{0:T(1024)S(1)}, f32[4,512]{1,0:T(4,128)S(1)}, f32[4,512]{1,0:T(4,128)S(1)}, /*index=5*/f32[4,34...) while((s32[]{:T(128)}, f32[1024]{0:T(1024)S(1)}, f32[1024]{0:T(1024)S(1)}, ...), condition=%wide.region_15.16_spmd.clone, body=%wide.region_12.15_spmd.clone.sunk | while | flops 217584640 | bytes 4505712 | solution.py:226
  256.3 2.1 fusion.113
  258.4 0.3 exponential_reduce_fusion.5
  258.8 2.1 fusion.113
  261.0 0.3 exponential_reduce_fusion.5
  261.4 2.1 fusion.113
  263.5 0.3 exponential_reduce_fusion.5
  263.9 2.1 fusion.113
  266.1 0.3 exponential_reduce_fusion.5
  266.5 0.6 broadcast_in_dim.49
  267.1 30.7 %all-to-all-start.1 = ((f32[8,2,1024]{2,1,0:T(2,128)}), f32[8,2,1024]{2,1,0:T(2,128)S(1)}, u32[]{:S(2)}, u32[]{:S(2)}) async-start(f32[8,2,1024]{2,1,0:T(2,128)} %broadcast_in_dim.49), calls=%async_computation.1 | async-start | bytes 131072 | tf_op jit(solution)/shard_map/all_to_all | solution.py:28
  298.0 0.6 fusion.73
  298.6 4.1 %all-to-all-done.1 = f32[8,2,1024]{2,1,0:T(2,128)S(1)} async-done(((f32[8,2,1024]{2,1,0:T(2,128)}), f32[8,2,1024]{2,1,0:T(2,128)S(1)}, u32[]{:S(2)}, u32[]{:S(2)}) %all-to-all-start.1) | async-done | bytes 65568 | tf_op jit(solution)/shard_map/all_to_all | solution.py:28
  303.1 0.6 subtract_multiply_fusion.1
  (126 shorter events, 4.7 us)
Async XLA Ops:
  0.6 94.0 %copy-start = (f32[34,34]{1,0:T(8,128)S(1)}, f32[34,34]{1,0:T(8,128)}, u32[]{:S(2)}) copy-start(f32[34,34]{1,0:T(8,128)} %param.19) | copy-start | bytes 13876
  2.0 92.5 %all-to-all-start = ((f32[8,4,1024]{2,1,0:T(4,128)}), f32[8,4,1024]{2,1,0:T(4,128)S(1)}, u32[]{:S(2)}, u32[]{:S(2)}) async-start(f32[8,4,1024]{2,1,0:T(4,128)} %broadcast_in_dim.44), calls=%async_computation | async-start | bytes 262144 | tf_op jit(solution)/shard_map/all_to_all | solution.py:28
  93.4 1.0 copy-start.2
  93.8 1.2 copy-start.3
  212.9 0.6 copy-start.1
  267.1 35.6 %all-to-all-start.1 = ((f32[8,2,1024]{2,1,0:T(2,128)}), f32[8,2,1024]{2,1,0:T(2,128)S(1)}, u32[]{:S(2)}, u32[]{:S(2)}) async-start(f32[8,2,1024]{2,1,0:T(2,128)} %broadcast_in_dim.49), calls=%async_computation.1 | async-start | bytes 131072 | tf_op jit(solution)/shard_map/all_to_all | solution.py:28
where the time goes:
time: 304 us
  blocking collectives  206 us (68%)
  starting transfers between devices  40.8 us (13%)
  matrix products  36.9 us (12%)
  local copies, waits for them, and re-layouts  7.68 us (3%)
  other arithmetic  6.67 us (2%)
  waiting for transfers between devices  4.13 us (1%)
    psum x4, blocking collectives, by_axis(): return functools.reduce(lax.psum, axes, x)  98.4 us
    all_gather x1, blocking collectives, rows_first(): lax.all_gather(both, axis, axis=0, tiled=True)  77.8 us
    all_to_all x2, starting transfers between devices, sent_to_all(): return lax.all_to_all(copies, axis, split_axis=0, concat_axis=0, tiled=True)  40.8 us
    all_gather x2, blocking collectives, collected_together(): both, at, found = (lax.all_gather(jnp.concatenate(lines), axis), 0, {})  29.8 us
    dot_general x12, matrix products, contract_rank(): lax.dot_general(left_block, weighted, (((0,), (0,)), ((), ())), precision...  24.7 us
    dot_general x8, matrix products, contract_last(): lax.dot_general(former, latter, (((1,), (1,)), ((), ())), precision=HIGHE...  11.6 us
  transfers between devices with their start and end apart: 2, of which 1 were waited for; matrix products, arithmetic and copies ran while one was open for 2% of the time, Pallas kernels for 0%

commit v1 on v0

--- a/solution.py
+++ b/solution.py
@@ -15,7 +15,13 @@
 def rows_first(arrays, axis, dims):
     turned = [jnp.moveaxis(a, dim, 0) for a, dim in zip(arrays, dims)]
     both = jnp.concatenate([t.reshape(len(t), -1) for t in turned], axis=1)
-    filled, at, gathered = (lax.all_gather(both, axis, axis=0, tiled=True), 0, [])
+    filled, at, gathered = (
+        jnp.concatenate(
+            lax.all_to_all(jnp.stack([both] * lax.axis_size(axis)), axis, 0, 0), axis=0
+        ),
+        0,
+        [],
+    )
     for t, dim in zip(turned, dims):
         slab = filled[:, at : at + t[0].size].reshape(-1, *t.shape[1:])
         gathered.append(jnp.moveaxis(slab, 0, dim))

time: 304 us -> 243 us (0.80)
  blocking collectives: 206 us -> 104 us
  waiting for transfers between devices: 4.13 us -> 25.9 us
  starting transfers between devices: 40.8 us -> 55.1 us
    all_gather x1 -> x0, blocking collectives: 77.8 us -> none  [rows_first(): lax.all_gather(both, axis, axis=0, tiled=True)]
    psum x4, blocking collectives: 98.4 us -> 74.8 us  [by_axis(): return functools.reduce(lax.psum, axes, x)]
    all_to_all x0 -> x1, waiting for transfers between devices: none -> 19.4 us  [rows_first(): lax.all_to_all(jnp.stack([both] * lax.axis_size(axis)), axis, 0, 0)]
    all_to_all x0 -> x1, starting transfers between devices: none -> 14.1 us  [rows_first(): lax.all_to_all(jnp.stack([both] * lax.axis_size(axis)), axis, 0, 0)]
  transfers between devices with their start and end apart: 2 -> 3, of which waited for: 1 -> 3; matrix products, arithmetic and copies ran while one was open for 2% -> 2% of each run, Pallas kernels for 0% -> 0%
where the time goes in v1:
time: 243 us; the launch traced here: 242 us
  blocking collectives  104 us (43%)
  starting transfers between devices  55.1 us (23%)
  matrix products  37 us (15%)
  waiting for transfers between devices  25.9 us (11%)
  local copies, waits for them, and re-layouts  10.7 us (4%)
  other arithmetic  7.56 us (3%)
    psum x4, blocking collectives, by_axis(): return functools.reduce(lax.psum, axes, x)  74.8 us
    all_to_all x2, starting transfers between devices, sent_to_all(): return lax.all_to_all(copies, axis, split_axis=0, concat_axis=0, tiled=True)  41 us
    all_gather x2, blocking collectives, collected_together(): both, at, found = (lax.all_gather(jnp.concatenate(lines), axis), 0, {})  29.4 us
    dot_general x12, matrix products, contract_rank(): lax.dot_general(left_block, weighted, (((0,), (0,)), ((), ())), precision...  24.7 us
    all_to_all x1, waiting for transfers between devices, rows_first(): lax.all_to_all(jnp.stack([both] * lax.axis_size(axis)), axis, 0, 0)  19.4 us
    all_to_all x1, starting transfers between devices, rows_first(): lax.all_to_all(jnp.stack([both] * lax.axis_size(axis)), axis, 0, 0)  14.1 us
    dot_general x8, matrix products, contract_last(): lax.dot_general(former, latter, (((1,), (1,)), ((), ())), precision=HIGHE...  11.6 us
    all_to_all x2, waiting for transfers between devices, sent_to_all(): return lax.all_to_all(copies, axis, split_axis=0, concat_axis=0, tiled=True)  6.47 us
  transfers between devices with their start and end apart: 3, of which 3 were waited for; matrix products, arithmetic and copies ran while one was open for 2% of the time, Pallas kernels for 0%

profile of v1, /device:TPU:1, one launch (start us, length us, event | category | flops | bytes accessed | tf_op | source)
XLA Modules:
  0.0 242.0 jit_solution(16196104918787123338)
XLA Ops:
  0.7 1.4 broadcast_in_dim.44
  2.1 10.1 %all-to-all-start.1 = ((f32[8,4,1024]{2,1,0:T(4,128)}), f32[8,4,1024]{2,1,0:T(4,128)S(1)}, u32[]{:S(2)}, u32[]{:S(2)}) async-start(f32[8,4,1024]{2,1,0:T(4,128)} %broadcast_in_dim.44), calls=%async_computation.1 | async-start | bytes 262144 | tf_op jit(solution)/shard_map/all_to_all | solution.py:34
  12.2 0.8 pad_maximum_fusion.4
  13.1 2.0 reshape.553
  15.1 2.3 all-to-all-done.1
  17.4 14.1 %all-to-all-start = ((f32[64,1,1088]{2,1,0:T(1,128)}), f32[64,1,1088]{2,1,0:T(1,128)S(1)}, u32[]{:S(2)}, u32[]{:S(2)}) async-start(f32[64,1,1088]{2,1,0:T(1,128)} %reshape.553), calls=%async_computation | async-start | bytes 589824 | tf_op jit(solution)/shard_map/all_to_all | solution.py:20
  32.1 19.4 %all-to-all-done = f32[64,1,1088]{2,1,0:T(1,128)S(1)} async-done(((f32[64,1,1088]{2,1,0:T(1,128)}), f32[64,1,1088]{2,1,0:T(1,128)S(1)}, u32[]{:S(2)}, u32[]{:S(2)}) %all-to-all-start) | async-done | bytes 278560 | tf_op jit(solution)/shard_map/all_to_all | solution.py:20
  51.5 0.5 broadcast.178
  52.0 1.3 reduce.136
  53.4 1.3 reshape.554
  54.7 0.9 slice_reduce_fusion
  57.0 19.6 %while.37 = (s32[]{:T(128)}, f32[34,34]{1,0:T(8,128)S(1)}, f32[4,34,512]{2,0,1:T(4,128)S(1)}, f32[4,512]{1,0:T(4,128)S(1)}, f32[1024]{0:T(1024)S(1)}, /*index=5*...) while((s32[]{:T(128)}, f32[34,34]{1,0:T(8,128)S(1)}, ...), condition=%wide.region_3.4_spmd.clone, body=%wide.region_2.3_spmd.clone.sunk | while | flops 438069504 | bytes 4957355 | solution.py:192
  57.1 1.8 fusion.109
  58.9 2.7 %fusion.110 = f32[512,34]{0,1:T(8,128)S(1)} fusion(f32[34,1024]{1,0:T(8,128)S(1)} %get-tuple-element.595, f32[512,1024]{1,0:T(8,128)S(1)} %fusion.109, f32[1024]{0:T(1024)S(1)} %get-tuple-element.592, f32[512]{0:T(512)S(1)} %bitcast.241, f32[1024]{0:T(1024)S(1)} %get-tuple-element.590, f32[512]{0:T(512)S(1)} %bitcast.242), kind=kOutput, calls=%fused_computation.5.clone.1 | convolution fusion | flops 217055232 | bytes 2318336 | tf_op jit(solution)/shard_map/while/body/eval_jaxpr/dot_general | solution.py:128
  62.0 1.9 fusion.109
  63.8 2.7 %fusion.110 = f32[512,34]{0,1:T(8,128)S(1)} fusion(f32[34,1024]{1,0:T(8,128)S(1)} %get-tuple-element.595, f32[512,1024]{1,0:T(8,128)S(1)} %fusion.109, f32[1024]{0:T(1024)S(1)} %get-tuple-element.592, f32[512]{0:T(512)S(1)} %bitcast.241, f32[1024]{0:T(1024)S(1)} %get-tuple-element.590, f32[512]{0:T(512)S(1)} %bitcast.242), kind=kOutput, calls=%fused_computation.5.clone.1 | convolution fusion | flops 217055232 | bytes 2318336 | tf_op jit(solution)/shard_map/while/body/eval_jaxpr/dot_general | solution.py:128
  66.9 1.9 fusion.109
  68.7 2.7 %fusion.110 = f32[512,34]{0,1:T(8,128)S(1)} fusion(f32[34,1024]{1,0:T(8,128)S(1)} %get-tuple-element.595, f32[512,1024]{1,0:T(8,128)S(1)} %fusion.109, f32[1024]{0:T(1024)S(1)} %get-tuple-element.592, f32[512]{0:T(512)S(1)} %bitcast.241, f32[1024]{0:T(1024)S(1)} %get-tuple-element.590, f32[512]{0:T(512)S(1)} %bitcast.242), kind=kOutput, calls=%fused_computation.5.clone.1 | convolution fusion | flops 217055232 | bytes 2318336 | tf_op jit(solution)/shard_map/while/body/eval_jaxpr/dot_general | solution.py:128
  71.7 1.9 fusion.109
  73.6 2.7 %fusion.110 = f32[512,34]{0,1:T(8,128)S(1)} fusion(f32[34,1024]{1,0:T(8,128)S(1)} %get-tuple-element.595, f32[512,1024]{1,0:T(8,128)S(1)} %fusion.109, f32[1024]{0:T(1024)S(1)} %get-tuple-element.592, f32[512]{0:T(512)S(1)} %bitcast.241, f32[1024]{0:T(1024)S(1)} %get-tuple-element.590, f32[512]{0:T(512)S(1)} %bitcast.242), kind=kOutput, calls=%fused_computation.5.clone.1 | convolution fusion | flops 217055232 | bytes 2318336 | tf_op jit(solution)/shard_map/while/body/eval_jaxpr/dot_general | solution.py:128
  76.6 11.8 %psum.28 = f32[34,34]{1,0:T(8,128)S(1)} all-reduce(f32[34,34]{1,0:T(8,128)S(1)} %get-tuple-element.131), channel_id=1, replica_groups=mesh['src_0'=4,'src_1'=2,'tgt_0'=4,'tgt_1'=16] {'src_0'}, use_global_device_ids=true, to_apply=%region_4.5 | all-reduce | flops 1156 | bytes 9248 | tf_op jit(solution)/shard_map/psum | solution.py:49
  88.5 10.1 %psum.29 = f32[34,34]{1,0:T(8,128)S(1)} all-reduce(f32[34,34]{1,0:T(8,128)S(1)} %psum.28), channel_id=1, replica_groups=mesh['src_0'=4,'src_1'=2,'tgt_0'=4,'tgt_1'=16] {'src_1'}, use_global_device_ids=true, to_apply=%region_5.6 | all-reduce | flops 1156 | bytes 9248 | tf_op jit(solution)/shard_map/psum | solution.py:49
  98.5 13.3 %psum.30 = f32[34,34]{1,0:T(8,128)S(1)} all-reduce(f32[34,34]{1,0:T(8,128)S(1)} %psum.29), channel_id=1, replica_groups=mesh['src_0'=4,'src_1'=2,'tgt_0'=4,'tgt_1'=16] {'tgt_0'}, use_global_device_ids=true, to_apply=%region_6.7 | all-reduce | flops 1156 | bytes 9248 | tf_op jit(solution)/shard_map/psum | solution.py:49
  111.8 39.6 %psum.31 = f32[34,34]{1,0:T(8,128)S(1)} all-reduce(f32[34,34]{1,0:T(8,128)S(1)} %psum.30), channel_id=1, replica_groups=mesh['src_0'=4,'src_1'=2,'tgt_0'=4,'tgt_1'=16] {'tgt_1'}, use_global_device_ids=true, to_apply=%region_7.8 | all-reduce | flops 1156 | bytes 9248 | tf_op jit(solution)/shard_map/psum | solution.py:49
  152.0 11.3 %while.36 = (s32[]{:T(128)}, f32[4,512]{1,0:T(4,128)S(1)}, f32[4,512]{1,0:T(4,128)S(1)}, f32[1024]{0:T(1024)S(1)}, f32[1024]{0:T(1024)S(1)}, /*index=5*/f32[4,34...) while((s32[]{:T(128)}, f32[4,512]{1,0:T(4,128)S(1)}, f32[4,512]{1,0:T(4,128)S(1)}, ...), condition=%wide.region_11.12_spmd, body=%wide.region_8.11_spmd.sunk | while | flops 217578496 | bytes 4462697 | solution.py:208
  152.0 2.2 fusion.103
  154.2 0.5 exponential_reduce_fusion.4
  154.9 2.2 fusion.103
  157.1 0.5 exponential_reduce_fusion.4
  157.7 2.2 fusion.103
  159.9 0.5 exponential_reduce_fusion.4
  160.5 2.2 fusion.103
  162.7 0.5 exponential_reduce_fusion.4
  163.4 9.0 %all-gather.2 = f32[4,2,2048]{2,1,0:T(2,128)S(1)} all-gather(f32[1,2,2048]{2,1,0:T(2,128)S(1)} %maximum_bitcast_fusion.2), channel_id=2, replica_groups=mesh['src_0'=4,'src_1'=2,'tgt_0'=4,'tgt_1'=16] {'tgt_0'}, dimensions={0}, use_global_device_ids=true | all-gather | bytes 81920 | tf_op jit(solution)/shard_map/all_gather | solution.py:60
  172.5 20.4 %all-gather.3 = f32[16,2,2048]{2,1,0:T(2,128)S(1)} all-gather(f32[1,2,2048]{2,1,0:T(2,128)S(1)} %maximum_bitcast_fusion.3), channel_id=3, replica_groups=mesh['src_0'=4,'src_1'=2,'tgt_0'=4,'tgt_1'=16] {'tgt_1'}, dimensions={0}, use_global_device_ids=true | all-gather | bytes 278528 | tf_op jit(solution)/shard_map/all_gather | solution.py:60
  192.9 0.4 slice_reduce_fusion.16
  193.3 0.3 slice_reduce_fusion.14
  194.4 10.2 %while.38 = (s32[]{:T(128)}, f32[1024]{0:T(1024)S(1)}, f32[1024]{0:T(1024)S(1)}, f32[4,512]{1,0:T(4,128)S(1)}, f32[4,512]{1,0:T(4,128)S(1)}, /*index=5*/f32[4,34...) while((s32[]{:T(128)}, f32[1024]{0:T(1024)S(1)}, f32[1024]{0:T(1024)S(1)}, ...), condition=%wide.region_15.16_spmd.clone, body=%wide.region_12.15_spmd.clone.sunk | while | flops 217584640 | bytes 4505712 | solution.py:232
  194.4 2.1 fusion.112
  196.6 0.3 exponential_reduce_fusion.5
  197.0 2.1 fusion.112
  199.5 2.1 fusion.112
  202.1 2.1 fusion.112
  204.6 0.6 broadcast_in_dim.49
  205.2 30.9 %all-to-all-start.2 = ((f32[8,2,1024]{2,1,0:T(2,128)}), f32[8,2,1024]{2,1,0:T(2,128)S(1)}, u32[]{:S(2)}, u32[]{:S(2)}) async-start(f32[8,2,1024]{2,1,0:T(2,128)} %broadcast_in_dim.49), calls=%async_computation.2 | async-start | bytes 131072 | tf_op jit(solution)/shard_map/all_to_all | solution.py:34
  236.3 0.6 fusion.71
  236.9 4.1 %all-to-all-done.2 = f32[8,2,1024]{2,1,0:T(2,128)S(1)} async-done(((f32[8,2,1024]{2,1,0:T(2,128)}), f32[8,2,1024]{2,1,0:T(2,128)S(1)}, u32[]{:S(2)}, u32[]{:S(2)}) %all-to-all-start.2) | async-done | bytes 65568 | tf_op jit(solution)/shard_map/all_to_all | solution.py:34
  241.4 0.6 subtract_multiply_fusion.1
  (132 shorter events, 6.5 us)
Async XLA Ops:
  0.6 31.2 %copy-start = (f32[34,34]{1,0:T(8,128)S(1)}, f32[34,34]{1,0:T(8,128)}, u32[]{:S(2)}) copy-start(f32[34,34]{1,0:T(8,128)} %param.19) | copy-start | bytes 13876
  0.6 31.0 %copy-start.2 = (f32[1024]{0:T(1024)S(1)}, f32[1024]{0:T(1024)}, u32[]{:S(2)}) copy-start(f32[1024]{0:T(1024)} %param.18) | copy-start | bytes 12292
  2.1 15.4 %all-to-all-start.1 = ((f32[8,4,1024]{2,1,0:T(4,128)}), f32[8,4,1024]{2,1,0:T(4,128)S(1)}, u32[]{:S(2)}, u32[]{:S(2)}) async-start(f32[8,4,1024]{2,1,0:T(4,128)} %broadcast_in_dim.44), calls=%async_computation.1 | async-start | bytes 262144 | tf_op jit(solution)/shard_map/all_to_all | solution.py:34
  17.4 34.1 %all-to-all-start = ((f32[64,1,1088]{2,1,0:T(1,128)}), f32[64,1,1088]{2,1,0:T(1,128)S(1)}, u32[]{:S(2)}, u32[]{:S(2)}) async-start(f32[64,1,1088]{2,1,0:T(1,128)} %reshape.553), calls=%async_computation | async-start | bytes 589824 | tf_op jit(solution)/shard_map/all_to_all | solution.py:20
  55.9 1.1 copy-start.3
  151.4 0.6 copy-start.1
  205.2 35.8 %all-to-all-start.2 = ((f32[8,2,1024]{2,1,0:T(2,128)}), f32[8,2,1024]{2,1,0:T(2,128)S(1)}, u32[]{:S(2)}, u32[]{:S(2)}) async-start(f32[8,2,1024]{2,1,0:T(2,128)} %broadcast_in_dim.49), calls=%async_computation.2 | async-start | bytes 131072 | tf_op jit(solution)/shard_map/all_to_all | solution.py:34
